TPU v7x, 128 devices: a whole 4x4x4 slice. The times are simulated.
128 devices in a mesh: fsdp: 32 (over y, x, core), model: 4 (over z).
Axes of the slice: x: 4, y: 4, z: 4, core: 2. Of those that a mesh axis runs over, the one named last changes fastest.
Arguments:
- w_query: float32 [4096, 4096], P('fsdp', 'model'), may hold values from -0.1875 to 0.1875
- first_query: float32 [4096, 4096], P('fsdp', 'model'), may hold values from -0.09375 to 0.09375
- second_query: float32 [4096, 4096], P('fsdp', 'model'), may hold values from -0.09375 to 0.09375
- w_key: float32 [4096, 4096], P('fsdp', 'model'), may hold values from -0.1875 to 0.1875
- first_key: float32 [4096, 4096], P('fsdp', 'model'), may hold values from -0.09375 to 0.09375
- second_key: float32 [4096, 4096], P('fsdp', 'model'), may hold values from -0.09375 to 0.09375
- w_value: float32 [4096, 4096], P('fsdp', 'model'), may hold values from -0.1875 to 0.1875
- first_value: float32 [4096, 4096], P('fsdp', 'model'), may hold values from -0.09375 to 0.09375
- second_value: float32 [4096, 4096], P('fsdp', 'model'), may hold values from -0.09375 to 0.09375
- norm_gain: float32 [4096], P('fsdp'), may hold values from 0.25 to 1.75
Outputs:
- ready_query: bfloat16 [4096, 4096], P(None, 'model')
- ready_key: bfloat16 [4096, 4096], P(None, 'model')
- ready_value: bfloat16 [4096, 4096], P(None, 'model')
- factor_query: float32 [4096], P('model')
- factor_key: float32 [4096], P('model')
- factor_value: float32 [4096], P('model')
All inputs are finite; a program needn't handle non-finite values. Where the computation divides by a largest or mean magnitude, that divisor is 1e-20 or more.
Results may differ from a plain program's by a relative error of at most 0.001.
Values may be sent and summed in bfloat16 or wider, within the bound.
A program may use at most 128 MiB of HBM per device.

v0:
```python
import jax
import jax.numpy as jnp
from jax import lax
from jax.sharding import PartitionSpec as P

D_MODEL = 4096


learn_rate = 0.2
hold_rate = 0.9


def from_everyone(value, axis):
    copies = jnp.broadcast_to(value, (lax.axis_size(axis), *value.shape))
    return lax.all_to_all(copies, axis, split_axis=0, concat_axis=0, tiled=True)


def of_everyone(value, axis):
    return from_everyone(value, axis).sum(axis=0)


def together(arrays, axis):
    ravelled, at, finished = (jnp.concatenate([a.reshape(-1) for a in arrays]), 0, [])
    total = of_everyone(ravelled, axis)
    for a in arrays:
        finished.append(total[at : at + a.size].reshape(a.shape))
        at += a.size
    return tuple(finished)


def sent_together(arrays, axis, dim, along):
    widths = [a.shape[along] for a in arrays]
    both = jnp.concatenate(arrays, axis=along)
    out = lax.all_gather(both, axis, axis=dim, tiled=True)
    return tuple(jnp.split(out, [sum(widths[:k]) for k in range(1, len(widths))], axis=along))


def on_device(
    w_query,
    first_query,
    second_query,
    w_key,
    first_key,
    second_key,
    w_value,
    first_value,
    second_value,
    norm_gain,
):
    hold_query = hold_rate * first_query + second_query
    latest_query = w_query - learn_rate * hold_query
    hold_key = hold_rate * first_key + second_key
    latest_key = w_key - learn_rate * hold_key
    hold_value = hold_rate * first_value + second_value
    latest_value = w_value - learn_rate * hold_value
    latest_gained_query = latest_query * norm_gain[:, None]
    latest_gained_key = latest_key * norm_gain[:, None]
    latest_gained_value = latest_value * norm_gain[:, None]
    total_query, total_key, total_value = together(
        (
            jnp.sum(jnp.abs(latest_gained_query), axis=0),
            jnp.sum(jnp.abs(latest_gained_key), axis=0),
            jnp.sum(jnp.abs(latest_gained_value), axis=0),
        ),
        "fsdp",
    )
    factor_query = total_query / D_MODEL
    factor_key = total_key / D_MODEL
    factor_value = total_value / D_MODEL
    narrow_query, narrow_key, narrow_value = (
        (latest_gained_query / factor_query).astype(jnp.bfloat16),
        (latest_gained_key / factor_key).astype(jnp.bfloat16),
        (latest_gained_value / factor_value).astype(jnp.bfloat16),
    )
    ready_query, ready_key, ready_value = sent_together(
        (narrow_query, narrow_key, narrow_value), "fsdp", 0, 1
    )
    return (ready_query, ready_key, ready_value, factor_query, factor_key, factor_value)


def solution(mesh):
    return jax.shard_map(
        on_device,
        mesh=mesh,
        in_specs=(
            P("fsdp", "model"),
            P("fsdp", "model"),
            P("fsdp", "model"),
            P("fsdp", "model"),
            P("fsdp", "model"),
            P("fsdp", "model"),
            P("fsdp", "model"),
            P("fsdp", "model"),
            P("fsdp", "model"),
            P("fsdp"),
        ),
        out_specs=(
            P(None, "model"),
            P(None, "model"),
            P(None, "model"),
            P("model"),
            P("model"),
            P("model"),
        ),
        check_vma=False,
    )
```

profile of v0, /device:TPU:1, one launch (start us, length us, event | category | flops | bytes accessed | tf_op | source)
XLA Modules:
  0.0 144.9 jit_solution(358993806925228647)
XLA Ops:
  7.2 0.0 all-gather.2.cloned.1.call-start
  7.2 2.9 %abs_reduce_fusion.2 = (f32[1024]{0:T(1024)S(1)}, f32[128,1024]{1,0:T(8,128)S(1)}, f32[1024]{0:T(1024)S(1)}, f32[128,1024]{1,0:T(8,128)S(1)}, f32[1024]{0:T(1024)S(1)}, /*index=5*/f32[128,1024]{1,0:T(8,128)S(1)}) fusion(f32[128]{0:T(128)} %param.19, f32[128,1024]{1,0:T(8,128)} %param.10, f32[128,1024]{1,0:T(8,128)} %param.12, f32[128,1024]{1,0:T(8,128)} %param.11, ...), kind=kLoop, calls=%fused_computation.8 | loop fusion | flops 2749440 | bytes 6304256 | tf_op jit(solution)/shard_map/reduce_sum | solution.py:61
  10.2 0.2 broadcast_in_dim.2
  10.4 18.5 %all_to_all.6 = f32[32,1,3072]{2,1,0:T(1,128)S(1)} all-to-all(f32[32,1,3072]{2,1,0:T(1,128)S(1)} %broadcast_in_dim.2), channel_id=1, replica_groups=mesh['fsdp'=32,'model'=4] {'fsdp'}, dimensions={0} | all-to-all | bytes 786432 | tf_op jit(solution)/shard_map/all_to_all | solution.py:15
  28.9 0.2 reduce_sum.39
  29.2 0.0 copy-start
  29.2 0.0 copy-start.1
  29.2 0.0 copy-start.2
  29.3 0.1 divide_convert_fusion
  29.4 0.9 pad_maximum_fusion
  30.3 0.0 all-gather.2.cloned.1.call-update
  30.3 90.7 %all-gather.2.cloned.1.call-done = bf16[4096,3072]{1,0:T(8,128)(2,1)} async-done(((bf16[128,3072]{1,0:T(8,128)(2,1)}), bf16[4096,3072]{1,0:T(8,128)(2,1)}) %all-gather.2.cloned.1.call-update) | async-done | bytes 25165840 | tf_op jit(solution)/shard_map/all_gather | solution.py:34
  121.0 17.0 %fusion = (bf16[4096,1024]{1,0:T(8,128)(2,1)}, bf16[4096,1024]{1,0:T(8,128)(2,1)}, bf16[4096,1024]{1,0:T(8,128)(2,1)}) fusion(bf16[4096,3072]{1,0:T(8,128)(2,1)} %all-gather.2.cloned.1.call-done), kind=kLoop, calls=%fused_computation.14 | loop fusion | bytes 50331648 | tf_op jit(solution)/shard_map/split | solution.py:35
  138.0 0.0 copy-done
  138.0 0.0 copy-done.1
  138.0 0.0 copy-done.2
  (3 shorter events, 0.1 us)
Async XLA Ops:
  7.2 113.8 %all-gather.2.cloned.1.call-start = ((), (), s32[]{:S(2)}) async-start(), calls=%async_computation.1 | async-start | bytes 25952256 | tf_op jit(solution)/shard_map/all_gather | solution.py:34
  29.2 108.9 %copy-start = (f32[1024]{0:T(1024)}, f32[1024]{0:T(1024)S(1)}, u32[]{:S(2)}) copy-start(f32[1024]{0:T(1024)S(1)} %get-tuple-element.15) | copy-start | bytes 12292
  29.2 108.8 %copy-start.1 = (f32[1024]{0:T(1024)}, f32[1024]{0:T(1024)S(1)}, u32[]{:S(2)}) copy-start(f32[1024]{0:T(1024)S(1)} %get-tuple-element.16) | copy-start | bytes 12292
  29.2 108.8 %copy-start.2 = (f32[1024]{0:T(1024)}, f32[1024]{0:T(1024)S(1)}, u32[]{:S(2)}) copy-start(f32[1024]{0:T(1024)S(1)} %get-tuple-element.17) | copy-start | bytes 12292
Sparse Core Ops, SparseCore 0:
  30.4 90.5 all-gather.1
where the time goes:
time: 145 us
  waiting for transfers between devices  90.7 us (63%)
  blocking collectives  18.5 us (13%)
  local copies, waits for them, and re-layouts  17.2 us (12%)
  between operations  14.1 us (10%)
  other arithmetic  4.27 us (3%)
    all_gather x1, waiting for transfers between devices, sent_together(): out = lax.all_gather(both, axis, axis=dim, tiled=True)  90.7 us
    all_to_all x1, blocking collectives, from_everyone(): return lax.all_to_all(copies, axis, split_axis=0, concat_axis=0, tiled=True)  18.5 us
    split x1, local copies, waits for them, and re-layouts, sent_together(): jnp.split(out, [sum(widths[:k]) for k in range(1, len(widths))], axis=along)  17 us
    reduce_sum x1, other arithmetic, on_device(): jnp.sum(jnp.abs(latest_gained_query), axis=0)  2.95 us
  transfers between devices with their start and end apart: 1, of which 1 were waited for; matrix products, arithmetic and copies ran while one was open for 0% of the time, Pallas kernels for 0%

commit v1 on v0

v1 whole, which is shorter than its diff:
```python
import jax
import jax.numpy as jnp
from jax import lax
from jax.experimental import pallas as pl
from jax.experimental.pallas import tpu as pltpu
from jax.sharding import PartitionSpec as P

MESH = pl.DeviceIdType.MESH
D_MODEL = 4096
learn_rate = 0.2
hold_rate = 0.9

KINDS = 3
SIDE = 4
LANES = 128
QUARTER = 4


def arrivals():
    names = []
    for sign in (-1, 1):
        for half in (0, 1):
            names.append(("near", sign, half))
    for half in (0, 1):
        names.append(("far", 0, half))
    for first in (0, -1, 1, 2):
        for sign in (-1, 1):
            for half in (0, 1):
                names.append(("near2", first, sign, half))
        for half in (0, 1):
            names.append(("far2", first, 0, half))
    return names


NAMES = arrivals()
INDEX = {(color, name): color * len(NAMES) + k for color in (0, 1) for k, name in enumerate(NAMES)}
N_LINK = 2 * len(NAMES)
OWN = {(color, half): N_LINK + 2 * color + half for color in (0, 1) for half in (0, 1)}
N_PAIR = N_LINK + 4


def gather_kernel(
    wq, fq, sq, wk, fk, sk, wv, fv, sv, gain_ref,
    out, factor_ref,
    staged, gained, gain_row, gain_full, sums, every, mine, other,
    in_sem, sum_send, sum_recv, pair_send, pair_recv, link_send, link_recv, d2d_send, d2d_recv,
):
    me = lax.axis_index("fsdp")
    core = lax.rem(me, 2)
    chip = me // 2
    x = lax.rem(chip, SIDE)
    y = chip // SIDE
    rows = gained.shape[1]
    columns = gained.shape[2]
    n_col = columns // LANES
    piece = rows // QUARTER

    def device(dy, dx):
        return (lax.rem(y + dy + SIDE, SIDE) * SIDE + lax.rem(x + dx + SIDE, SIDE)) * 2 + core

    partner = chip * 2 + 1 - core

    loads = []
    for k, ref in enumerate((wq, fq, sq, wk, fk, sk, wv, fv, sv)):
        loads.append(pltpu.make_async_copy(ref, staged.at[k], in_sem.at[k]))
    loads.append(pltpu.make_async_copy(gain_ref, gain_row, in_sem.at[9]))
    loads[9].start()
    for k in range(9):
        loads[k].start()

    barrier = pltpu.get_barrier_semaphore()
    pl.semaphore_signal(barrier, inc=1, device_id={"fsdp": partner}, device_id_type=MESH)
    for k in range(1, SIDE * SIDE):
        pl.semaphore_signal(
            barrier, inc=1, device_id={"fsdp": device(k // SIDE, k % SIDE)}, device_id_type=MESH
        )

    loads[9].wait()
    gain_full[...] = jnp.broadcast_to(gain_row[...], (rows, rows)).T
    for m in range(KINDS):
        for k in range(3):
            loads[3 * m + k].wait()
        for j in range(n_col):
            at = slice(j * LANES, (j + 1) * LANES)
            hold = hold_rate * staged[3 * m + 1, :, at] + staged[3 * m + 2, :, at]
            latest = staged[3 * m, :, at] - learn_rate * hold
            value = latest * gain_full[...]
            gained[m, :, at] = value
            sums[m * n_col + j : m * n_col + j + 1, :] = jnp.sum(jnp.abs(value), axis=0, keepdims=True)

    pl.semaphore_wait(barrier, SIDE * SIDE)

    def sum_copy(k):
        return pltpu.make_async_remote_copy(
            src_ref=sums,
            dst_ref=every.at[chip],
            send_sem=sum_send.at[k],
            recv_sem=sum_recv.at[k],
            device_id={"fsdp": device(k // SIDE, k % SIDE)},
            device_id_type=MESH,
        )

    for k in (10, 11, 9, 14, 6, 2, 8, 5, 7, 13, 15, 1, 3, 4, 12):
        sum_copy(k).start()
    every[chip] = sums[...]
    for k in range(1, SIDE * SIDE):
        sum_copy(k).wait_recv()
    total = every[0]
    for k in range(1, SIDE * SIDE):
        total = total + every[k]
    mine[...] = total
    pair = pltpu.make_async_remote_copy(
        src_ref=mine,
        dst_ref=other,
        send_sem=pair_send,
        recv_sem=pair_recv,
        device_id={"fsdp": partner},
        device_id_type=MESH,
    )
    pair.start()
    pair.wait_recv()
    factor_ref[...] = (mine[...] + other[...]) / D_MODEL
    mine_recip = 1.0 / factor_ref[...]

    def block_start(color, first, second):
        dy, dx = (second, first) if color == 0 else (first, second)
        return device(dy, dx) * rows

    def place(color, first, second, half):
        at = pl.multiple_of(block_start(color, first, second) + (2 * color + half) * piece, piece)
        return out.at[:, pl.ds(at, piece), :]

    def neighbour(color, stage, sign):
        along_x = (color == 0) == (stage == 1)
        return device(0, sign) if along_x else device(sign, 0)

    def where(color, name):
        if name[0] == "near":
            return name[1], 0
        if name[0] == "far":
            return 2, 0
        if name[0] == "near2":
            return name[1], name[2]
        return name[1], 2

    sent = []

    def link(color, name, first, second, target):
        half = name[-1]
        k = INDEX[(color, name)]
        ref = place(color, first, second, half)
        return pltpu.make_async_remote_copy(
            src_ref=ref,
            dst_ref=ref,
            send_sem=link_send.at[k],
            recv_sem=link_recv.at[k],
            device_id={"fsdp": target},
            device_id_type=MESH,
        )

    def send(color, name, first, second, stage, sign):
        copy = link(color, name, first, second, neighbour(color, stage, sign))
        copy.start()
        sent.append(copy)

    def to_partner(k, color, first, second, half):
        ref = place(color, first, second, half)
        copy = pltpu.make_async_remote_copy(
            src_ref=ref,
            dst_ref=ref,
            send_sem=d2d_send.at[k],
            recv_sem=d2d_recv.at[k],
            device_id={"fsdp": partner},
            device_id_type=MESH,
        )
        copy.start()
        sent.append(copy)

    def arrived(color, name):
        first, second = where(color, name)
        link(color, name, first, second, me).wait_recv()
        half = name[-1]
        kind = name[0]
        if kind == "near":
            sign = name[1]
            if (sign, half) in ((-1, 0), (1, 1)):
                send(color, ("far", 0, half), first, second, 1, -sign)
        if kind in ("near", "far"):
            for to in (1, -1):
                send(color, ("near2", first, -to, half), first, second, 2, to)
        if kind == "near2":
            sign = name[2]
            if (sign, half) in ((-1, 0), (1, 1)):
                send(color, ("far2", first, 0, half), first, second, 2, -sign)
        to_partner(INDEX[(color, name)], color, first, second, half)

    order = ((0, 0), (1, 0), (0, 1), (1, 1))
    for color, half in order:
        low = (2 * color + half) * piece
        at = pl.multiple_of(me * rows + low, piece)
        for m in range(KINDS):
            for j in range(n_col):
                cols = slice(j * LANES, (j + 1) * LANES)
                row = m * n_col + j
                out[m, pl.ds(at, piece), cols] = (
                    gained[m, low : low + piece, cols] * mine_recip[row : row + 1, :]
                ).astype(out.dtype)
    for color in (0, 1):
        for to in (1, -1):
            for half in ((0, 1) if to == 1 else (1, 0)):
                send(color, ("near", -to, half), 0, 0, 1, to)
    for color in (0, 1):
        for to in (1, -1):
            for half in ((0, 1) if to == 1 else (1, 0)):
                send(color, ("near2", 0, -to, half), 0, 0, 2, to)
    for color, half in order:
        to_partner(OWN[(color, half)], color, 0, 0, half)

    both = (0, 1)
    for name in (("near", -1, 0), ("near", 1, 1), ("near", -1, 1), ("near", 1, 0)):
        for color in both:
            arrived(color, name)
    for name in (("near2", 0, -1, 0), ("near2", 0, 1, 1), ("near2", 0, -1, 1), ("near2", 0, 1, 0)):
        for color in both:
            arrived(color, name)
    for name in (("far", 0, 0), ("far", 0, 1)):
        for color in both:
            arrived(color, name)
    for first in (-1, 1, 2):
        for half in ((0, 1) if first != 1 else (1, 0)):
            for sign in (-1, 1):
                for color in both:
                    arrived(color, ("near2", first, sign, half))
        if first == -1:
            for half in (0, 1):
                for color in both:
                    arrived(color, ("far2", 0, 0, half))
    for first in (-1, 1, 2):
        for half in (0, 1):
            for color in both:
                arrived(color, ("far2", first, 0, half))

    def from_partner(k, color, first, second, half):
        dy, dx = (second, first) if color == 0 else (first, second)
        at = (device(dy, dx) + 1 - 2 * core) * rows + (2 * color + half) * piece
        ref = out.at[:, pl.ds(pl.multiple_of(at, piece), piece), :]
        pltpu.make_async_remote_copy(
            src_ref=ref,
            dst_ref=ref,
            send_sem=d2d_send.at[k],
            recv_sem=d2d_recv.at[k],
            device_id={"fsdp": partner},
            device_id_type=MESH,
        ).wait_recv()

    for color in both:
        for half in (0, 1):
            from_partner(OWN[(color, half)], color, 0, 0, half)
        for name in NAMES:
            from_partner(INDEX[(color, name)], color, *where(color, name), name[-1])
    for copy in sent:
        copy.wait_send()
    for k in range(1, SIDE * SIDE):
        sum_copy(k).wait_send()
    pair.wait_send()


def store_kernel(whole, factors, oq, ok, ov, tq, tk, tv, sem, small):
    n_row = oq.shape[0]
    parts = 8
    step = n_row // parts
    copies = []
    for m, ref in enumerate((oq, ok, ov)):
        for k in range(parts):
            copies.append(
                pltpu.make_async_copy(
                    whole.at[m, k * step : (k + 1) * step, :],
                    ref.at[k * step : (k + 1) * step, :],
                    sem.at[m * parts + k],
                )
            )
    n_col = tq.shape[0]
    for m, ref in enumerate((tq, tk, tv)):
        copies.append(
            pltpu.make_async_copy(factors.at[m * n_col : (m + 1) * n_col, :], ref, small.at[m])
        )
    for copy in copies:
        copy.start()
    for copy in copies:
        copy.wait()


def on_device(*args):
    weights, gain = args[:9], args[9]
    rows, columns = weights[0].shape
    n_col = columns // LANES
    n = lax.axis_size("fsdp")
    f32, bf16 = jnp.float32, jnp.bfloat16
    anywhere = pl.BlockSpec(memory_space=pl.ANY)
    local = pl.BlockSpec(memory_space=pltpu.VMEM)
    dma = pltpu.SemaphoreType.DMA
    whole, factors = pl.pallas_call(
        gather_kernel,
        out_shape=(
            pltpu.VMEM((KINDS, n * rows, columns), bf16),
            pltpu.VMEM((KINDS * n_col, LANES), f32),
        ),
        in_specs=[anywhere] * 10,
        out_specs=(local, local),
        scratch_shapes=[
            pltpu.VMEM((9, rows, columns), f32),
            pltpu.VMEM((KINDS, rows, columns), f32),
            pltpu.VMEM((1, rows), f32),
            pltpu.VMEM((rows, rows), f32),
            pltpu.VMEM((KINDS * n_col, LANES), f32),
            pltpu.VMEM((SIDE * SIDE, KINDS * n_col, LANES), f32),
            pltpu.VMEM((KINDS * n_col, LANES), f32),
            pltpu.VMEM((KINDS * n_col, LANES), f32),
            dma((10,)),
            dma((SIDE * SIDE,)),
            dma((SIDE * SIDE,)),
            dma,
            dma,
            dma((N_LINK,)),
            dma((N_LINK,)),
            dma((N_PAIR,)),
            dma((N_PAIR,)),
        ],
        compiler_params=pltpu.CompilerParams(
            collective_id=0, has_side_effects=True, vmem_limit_bytes=36 * 2**20
        ),
        name="gather",
    )(*weights, gain.reshape(1, rows))
    tile = jax.ShapeDtypeStruct((n_col, LANES), f32)
    matrix = jax.ShapeDtypeStruct((n * rows, columns), bf16)
    q, k, v, tq, tk, tv = pl.pallas_call(
        store_kernel,
        out_shape=(matrix, matrix, matrix, tile, tile, tile),
        in_specs=[local, local],
        out_specs=(anywhere,) * 6,
        scratch_shapes=[dma((24,)), dma((3,))],
        compiler_params=pltpu.CompilerParams(vmem_limit_bytes=32 * 2**20),
        name="store",
    )(whole, factors)
    return (q, k, v, tq.reshape(-1), tk.reshape(-1), tv.reshape(-1))


def solution(mesh):
    return jax.shard_map(
        on_device,
        mesh=mesh,
        in_specs=(P("fsdp", "model"),) * 9 + (P("fsdp"),),
        out_specs=(P(None, "model"),) * 3 + (P("model"),) * 3,
        check_vma=False,
    )
```

time: 145 us -> 109 us (0.75)
  Pallas kernels: 0 us -> 99.4 us
  waiting for transfers between devices: 90.7 us -> 0 us
  blocking collectives: 18.5 us -> 0 us
  between operations: 14.1 us -> 0.65 us
  local copies, waits for them, and re-layouts: 17.2 us -> 8.3 us
  other arithmetic: 4.27 us -> 0 us
    pallas_call x0 -> x2, Pallas kernels: none -> 99.4 us  [the longest x1 82.7 us: on_device(): pl.pallas_call(gather_kernel, out_shape=(pltpu.VMEM((KINDS, n * rows, col...]
    all_gather x1 -> x0, waiting for transfers between devices: 90.7 us -> none  [sent_together(): out = lax.all_gather(both, axis, axis=dim, tiled=True)]
    all_to_all x1 -> x0, blocking collectives: 18.5 us -> none  [from_everyone(): return lax.all_to_all(copies, axis, split_axis=0, concat_axis=0, tiled=True)]
    split x1 -> x0, local copies, waits for them, and re-layouts: 17 us -> none  [sent_together(): jnp.split(out, [sum(widths[:k]) for k in range(1, len(widths))], axis=along)]
    unnamed x6 -> x2, local copies, waits for them, and re-layouts: 0.02 us -> 8.3 us
    reduce_sum x2 -> x0, other arithmetic: 3.18 us -> none  [the longest x1 2.95 us: on_device(): jnp.sum(jnp.abs(latest_gained_query), axis=0)]
  transfers between devices with their start and end apart: 1 -> 0, of which waited for: 1 -> 0; matrix products, arithmetic and copies ran while one was open for 0% -> 0% of each run, Pallas kernels for 0% -> 0%
where the time goes in v1:
time: 109 us; the launch traced here: 108 us
  Pallas kernels  99.4 us (91%)
  local copies, waits for them, and re-layouts  8.3 us (8%)
    pallas_call x1, Pallas kernels, on_device(): pl.pallas_call(gather_kernel, out_shape=(pltpu.VMEM((KINDS, n * rows, col...  82.7 us
    pallas_call x1, Pallas kernels, on_device(): pl.pallas_call(store_kernel, out_shape=(matrix, matrix, matrix, tile, til...  16.7 us
    unnamed x2, local copies, waits for them, and re-layouts  8.3 us

profile of v1, /device:TPU:1, one launch (start us, length us, event | category | flops | bytes accessed | tf_op | source)
XLA Modules:
  0.0 108.4 jit_solution(17841667688324323274)
XLA Ops:
  0.6 82.7 %gather.1 = (bf16[3,4096,1024]{2,1,0:T(8,128)(2,1)S(1)}, f32[24,128]{1,0:T(8,128)S(1)}) custom-call(f32[128,1024]{1,0:T(8,128)} %wq.1, f32[128,1024]{1,0:T(8,128)} %fq.1, f32[128,1024]{1,0:T(8,128)} %sq.1, f32[128,1024]{1,0:T(8,128)} %wk.1, f32[128,1024]{1,0:T(8,128)} %fk.1, f32[128,1024]{1,0:T(8,128)} %sk.1, f32[128,1024]{1,0:T(8,128)} %wv.1, ...), custom_call_target="tpu_custom_call" | custom-call | tf_op jit(solution)/shard_map/gather/pallas_call | solution.py:302
  83.3 0.0 copy-start
  83.3 8.3 %copy-done = bf16[3,4096,1024]{2,1,0:T(8,128)(2,1)} copy-done((bf16[3,4096,1024]{2,1,0:T(8,128)(2,1)}, bf16[3,4096,1024]{2,1,0:T(8,128)(2,1)S(1)}, u32[]{:S(2)}) %copy-start) | copy-done | bytes 25165848
  91.6 16.7 %store.1 = (bf16[4096,1024]{1,0:T(8,128)(2,1)}, bf16[4096,1024]{1,0:T(8,128)(2,1)}, bf16[4096,1024]{1,0:T(8,128)(2,1)}, f32[8,128]{1,0:T(8,128)}, f32[8,128]{1,0:T(8,128)}, /*index=5*/f32[8,128]{1,0:T(8,128)}) custom-call(bf16[3,4096,1024]{2,1,0:T(8,128)(2,1)} %copy-done, f32[24,128]{1,0:T(8,128)S(1)} %get-tuple-element.15.factors), custom_call_target="tpu_custom_call" | custom-call | tf_op jit(solution)/shard_map/store/pallas_call | solution.py:336
Async XLA Ops:
  83.3 8.3 %copy-start = (bf16[3,4096,1024]{2,1,0:T(8,128)(2,1)}, bf16[3,4096,1024]{2,1,0:T(8,128)(2,1)S(1)}, u32[]{:S(2)}) copy-start(bf16[3,4096,1024]{2,1,0:T(8,128)(2,1)S(1)} %get-tuple-element.14.whole) | copy-start | bytes 75497472

commit v2 on v1

--- a/solution.py
+++ b/solution.py
@@ -339,9 +339,12 @@
         in_specs=[local, local],
         out_specs=(anywhere,) * 6,
         scratch_shapes=[dma((24,)), dma((3,))],
-        compiler_params=pltpu.CompilerParams(vmem_limit_bytes=32 * 2**20),
+        compiler_params=pltpu.CompilerParams(vmem_limit_bytes=4 * 2**20),
         name="store",
-    )(whole, factors)
+    )(
+        pltpu.with_memory_space_constraint(whole, pltpu.VMEM),
+        pltpu.with_memory_space_constraint(factors, pltpu.VMEM),
+    )
     return (q, k, v, tq.reshape(-1), tk.reshape(-1), tv.reshape(-1))
 
 

time: 109 us -> 92 us (0.84)
  local copies, waits for them, and re-layouts: 8.3 us -> 0 us
  Pallas kernels: 99.4 us -> 91.3 us
    unnamed x2 -> x0, local copies, waits for them, and re-layouts: 8.3 us -> none
    pallas_call x1, Pallas kernels: 16.7 us -> 8.6 us  [on_device(): pl.pallas_call(store_kernel, out_shape=(matrix, matrix, matrix, tile, til...]
where the time goes in v2:
time: 92 us; the launch traced here: 91.9 us
  Pallas kernels  91.3 us (99%)
    pallas_call x1, Pallas kernels, on_device(): pl.pallas_call(gather_kernel, out_shape=(pltpu.VMEM((KINDS, n * rows, col...  82.7 us
    pallas_call x1, Pallas kernels, on_device(): pl.pallas_call(store_kernel, out_shape=(matrix, matrix, matrix, tile, til...  8.6 us

profile of v2, /device:TPU:1, one launch (start us, length us, event | category | flops | bytes accessed | tf_op | source)
XLA Modules:
  0.0 91.9 jit_solution(10833507361369248913)
XLA Ops:
  0.6 82.7 %gather.1 = (bf16[3,4096,1024]{2,1,0:T(8,128)(2,1)S(1)}, f32[24,128]{1,0:T(8,128)S(1)}) custom-call(f32[128,1024]{1,0:T(8,128)} %wq.1, f32[128,1024]{1,0:T(8,128)} %fq.1, f32[128,1024]{1,0:T(8,128)} %sq.1, f32[128,1024]{1,0:T(8,128)} %wk.1, f32[128,1024]{1,0:T(8,128)} %fk.1, f32[128,1024]{1,0:T(8,128)} %sk.1, f32[128,1024]{1,0:T(8,128)} %wv.1, ...), custom_call_target="tpu_custom_call" | custom-call | tf_op jit(solution)/shard_map/gather/pallas_call | solution.py:302
  83.3 8.6 %store.1 = (bf16[4096,1024]{1,0:T(8,128)(2,1)}, bf16[4096,1024]{1,0:T(8,128)(2,1)}, bf16[4096,1024]{1,0:T(8,128)(2,1)}, f32[8,128]{1,0:T(8,128)}, f32[8,128]{1,0:T(8,128)}, /*index=5*/f32[8,128]{1,0:T(8,128)}) custom-call(bf16[3,4096,1024]{2,1,0:T(8,128)(2,1)S(1)} %get-tuple-element.14.whole, f32[24,128]{1,0:T(8,128)S(1)} %get-tuple-element.15.factors), custom_call_target="tpu_custom_call" | custom-call | tf_op jit(solution)/shard_map/store/pallas_call | solution.py:336

commit v3 on v2

v3 whole, which is shorter than its diff:
```python
import jax
import jax.numpy as jnp
from jax import lax
from jax.experimental import pallas as pl
from jax.experimental.pallas import tpu as pltpu
from jax.sharding import PartitionSpec as P

MESH = pl.DeviceIdType.MESH
D_MODEL = 4096
learn_rate = 0.2
hold_rate = 0.9

KINDS = 3
SIDE = 4
LANES = 128
QUARTER = 4


LAST = 2
EARLY = 2


def arrivals():
    names = []
    for sign, half in ((-1, 1), (1, 0)):
        names.append(("near", sign, half))
    for half in (0, 1):
        names.append(("far", 0, half))
    for first in (0, -1, 1, 2):
        for sign in (-1, 1):
            for half in (0, 1):
                names.append(("near2", first, sign, half))
        for half in (0, 1):
            names.append(("far2", first, 0, half))
    table, at = {}, 0
    for color in (0, 1):
        for name in names:
            table[(color, name)] = at
            at += KINDS if name[:2] == ("far2", LAST) else 1
    return table, at, 2 * len(names)


INDEX, N_SEM, N_LINK = arrivals()
N_PAIR = N_LINK + 8


def gather_kernel(
    wq, fq, sq, wk, fk, sk, wv, fv, sv, gain_ref,
    out, factor_ref,
    staged, gained, early, gain_row, gain_full, sums, row_sums, every,
    in_sem, sum_send, row_recv, column_recv, early_send, early_recv, all_send, link_recv, d2d_recv,
):
    me = lax.axis_index("fsdp")
    core = lax.rem(me, 2)
    chip = me // 2
    x = lax.rem(chip, SIDE)
    y = chip // SIDE
    rows = gained.shape[1]
    columns = gained.shape[2]
    n_col = columns // LANES
    piece = rows // QUARTER

    def device(dy, dx, on=core):
        return (lax.rem(y + dy + SIDE, SIDE) * SIDE + lax.rem(x + dx + SIDE, SIDE)) * 2 + on

    partner = device(0, 0, 1 - core)
    row_peers = [partner] + [device(0, dx, on) for dx in (2, 1, 3) for on in (core, 1 - core)]
    column_peers = [device(dy, 0) for dy in (2, 1, 3)]

    barrier = pltpu.get_barrier_semaphore()
    for peer in column_peers + row_peers:
        pl.semaphore_signal(barrier, inc=1, device_id={"fsdp": peer}, device_id_type=MESH)

    weights = (wq, fq, sq, wk, fk, sk, wv, fv, sv)
    gain_load = pltpu.make_async_copy(gain_ref, gain_row, in_sem.at[KINDS])
    gain_load.start()
    for k, ref in enumerate(weights):
        pltpu.make_async_copy(ref, staged.at[k], in_sem.at[k // 3]).start()

    gain_load.wait()
    gain_full[...] = jnp.broadcast_to(gain_row[...], (rows, rows)).T
    for m in range(KINDS):
        all_three = staged.at[3 * m : 3 * m + 3]
        pltpu.make_async_copy(all_three, all_three, in_sem.at[m]).wait()
        for j in range(n_col):
            at = slice(j * LANES, (j + 1) * LANES)
            hold = hold_rate * staged[3 * m + 1, :, at] + staged[3 * m + 2, :, at]
            latest = staged[3 * m, :, at] - learn_rate * hold
            value = latest * gain_full[...]
            gained[m, :, at] = value
            sums[m * n_col + j : m * n_col + j + 1, :] = jnp.sum(jnp.abs(value), axis=0, keepdims=True)

    pl.semaphore_wait(barrier, len(row_peers) + len(column_peers))

    def neighbour(color, stage, sign):
        along_x = (color == 0) == (stage == 1)
        return device(0, sign) if along_x else device(sign, 0)

    part = piece // EARLY

    def early_copy(color, side, k):
        low = (2 * color + side) * piece + k * part
        return pltpu.make_async_remote_copy(
            src_ref=gained.at[:, low : low + part, :],
            dst_ref=early.at[color, side, k],
            send_sem=early_send,
            recv_sem=early_recv.at[(2 * color + side) * EARLY + k],
            device_id={"fsdp": neighbour(color, 1, 1 - 2 * side)},
            device_id_type=MESH,
        )

    n_row = 2 * SIDE

    def sum_copy(source, slot, recv_sem, target):
        return pltpu.make_async_remote_copy(
            src_ref=source,
            dst_ref=every.at[slot],
            send_sem=sum_send,
            recv_sem=recv_sem,
            device_id={"fsdp": target},
            device_id_type=MESH,
        )

    def wait_all(ref, sem):
        pltpu.make_async_copy(ref, ref, sem).wait()

    for peer in row_peers:
        sum_copy(sums, 2 * x + core, row_recv, peer).start()
    early_copy(1, 0, 0).start()
    early_copy(1, 1, 0).start()
    early_copy(0, 0, 0).start()
    early_copy(0, 1, 0).start()
    every[2 * x + core] = sums[...]
    wait_all(every.at[0 : n_row - 1], row_recv)
    total = every[0]
    for k in range(1, n_row):
        total = total + every[k]
    row_sums[...] = total
    for peer in column_peers:
        sum_copy(row_sums, n_row + y, column_recv, peer).start()
    early_copy(0, 0, 1).start()
    early_copy(0, 1, 1).start()
    early_copy(1, 0, 1).start()
    early_copy(1, 1, 1).start()
    every[n_row + y] = total
    wait_all(every.at[n_row : n_row + SIDE - 1], column_recv)
    total = every[n_row]
    for k in range(1, SIDE):
        total = total + every[n_row + k]
    factor_ref[...] = total / D_MODEL
    recip = 1.0 / factor_ref[...]

    def block_start(color, first, second):
        dy, dx = (second, first) if color == 0 else (first, second)
        return device(dy, dx) * rows

    def place(color, first, second, half):
        at = pl.multiple_of(block_start(color, first, second) + (2 * color + half) * piece, piece)
        return out.at[:, pl.ds(at, piece), :]

    def where(color, name):
        if name[0] == "near":
            return name[1], 0
        if name[0] == "far":
            return 2, 0
        if name[0] == "near2":
            return name[1], name[2]
        return name[1], 2

    def groups(name):
        if name[:2] == ("far2", LAST):
            return [(m, m + 1) for m in range(KINDS)]
        return [(0, KINDS)]

    def link(color, name, first, second, target, group):
        low, high = group
        ref = place(color, first, second, name[-1]).at[low:high]
        return pltpu.make_async_remote_copy(
            src_ref=ref,
            dst_ref=ref,
            send_sem=all_send,
            recv_sem=link_recv.at[INDEX[(color, name)] + low],
            device_id={"fsdp": target},
            device_id_type=MESH,
        )

    def send(color, name, first, second, stage, sign):
        for group in groups(name):
            link(color, name, first, second, neighbour(color, stage, sign), group).start()

    def to_partner(color, first, second, half, group=(0, KINDS)):
        ref = place(color, first, second, half).at[group[0] : group[1]]
        pltpu.make_async_remote_copy(
            src_ref=ref,
            dst_ref=ref,
            send_sem=all_send,
            recv_sem=d2d_recv,
            device_id={"fsdp": partner},
            device_id_type=MESH,
        ).start()

    def arrived(color, name, group=(0, KINDS)):
        first, second = where(color, name)
        link(color, name, first, second, partner, group).wait_recv()
        half = name[-1]
        if name[0] in ("near", "far"):
            first_axis_done(color, first, half)
        if name[0] == "near2" and (name[2], half) in ((-1, 0), (1, 1)):
            send(color, ("far2", first, 0, half), first, second, 2, -name[2])
        to_partner(color, first, second, half, group)

    def first_axis_done(color, first, half):
        for to in (1, -1) if half == 0 else (-1, 1):
            send(color, ("near2", first, -to, half), first, 0, 2, to)

    def scaled(color, first, half, source, low, count):
        start = block_start(color, first, 0) + (2 * color + half) * piece + low
        at = pl.multiple_of(start, count)
        for m in range(KINDS):
            for j in range(n_col):
                cols = slice(j * LANES, (j + 1) * LANES)
                row = m * n_col + j
                out[m, pl.ds(at, count), cols] = (
                    source(m, cols) * recip[row : row + 1, :]
                ).astype(out.dtype)

    both = (0, 1)
    halves = (0, 1)
    for half in halves:
        for color in both:
            low = (2 * color + half) * piece
            scaled(color, 0, half, lambda m, cols: gained[m, low : low + piece, cols], 0, piece)
    for half in halves:
        for color in both:
            to = 1 if half == 1 else -1
            send(color, ("near", -to, half), 0, 0, 1, to)
    for color in both:
        for side in halves:
            first = 2 * side - 1
            for k in range(EARLY):
                early_copy(color, side, k).wait_recv()
                scaled(color, first, side, lambda m, cols: early[color, side, k, m, :, cols], k * part, part)
    for half in halves:
        for color in both:
            first_axis_done(color, 0, half)
    for color in both:
        for side in halves:
            first = 2 * side - 1
            send(color, ("far", 0, side), first, 0, 1, -first)
    for color in both:
        for side in halves:
            first_axis_done(color, 2 * side - 1, side)
    for color in both:
        for half in halves:
            to_partner(color, 0, 0, half)
            to_partner(color, 2 * half - 1, 0, half)

    for name in (("near", -1, 1), ("near", 1, 0)):
        for color in both:
            arrived(color, name)
    for name in (("near2", 0, -1, 0), ("near2", 0, 1, 1), ("near2", 0, -1, 1), ("near2", 0, 1, 0)):
        for color in both:
            arrived(color, name)
    for name in (("far", 0, 0), ("far", 0, 1)):
        for color in both:
            arrived(color, name)
    for first in (-1, 1, 2):
        for half in ((0, 1) if first != 1 else (1, 0)):
            for sign in (-1, 1):
                for color in both:
                    arrived(color, ("near2", first, sign, half))
        if first == -1:
            for half in halves:
                for color in both:
                    arrived(color, ("far2", 0, 0, half))
    for first in (-1, 1, LAST):
        name = ("far2", first, 0)
        for group in groups(name):
            for half in halves:
                for color in both:
                    arrived(color, (*name, half), group)

    wait_all(out.at[:, 0 : N_PAIR * piece, :], d2d_recv)
    wait_all(out.at[:, 0 : (N_LINK + N_PAIR) * piece, :], all_send)
    wait_all(early, early_send)
    wait_all(every.at[0 : len(row_peers) + len(column_peers)], sum_send)


def store_kernel(whole, factors, oq, ok, ov, tq, tk, tv, sem, small):
    n_row = oq.shape[0]
    parts = 8
    step = n_row // parts
    copies = []
    for m, ref in enumerate((oq, ok, ov)):
        for k in range(parts):
            copies.append(
                pltpu.make_async_copy(
                    whole.at[m, k * step : (k + 1) * step, :],
                    ref.at[k * step : (k + 1) * step, :],
                    sem,
                )
            )
    n_col = tq.shape[0]
    for m, ref in enumerate((tq, tk, tv)):
        copies.append(
            pltpu.make_async_copy(factors.at[m * n_col : (m + 1) * n_col, :], ref, small)
        )
    for copy in copies:
        copy.start()
    pltpu.make_async_copy(whole, whole, sem).wait()
    pltpu.make_async_copy(factors, factors, small).wait()


def on_device(*args):
    weights, gain = args[:9], args[9]
    rows, columns = weights[0].shape
    n_col = columns // LANES
    n = lax.axis_size("fsdp")
    f32, bf16 = jnp.float32, jnp.bfloat16
    anywhere = pl.BlockSpec(memory_space=pl.ANY)
    local = pl.BlockSpec(memory_space=pltpu.VMEM)
    dma = pltpu.SemaphoreType.DMA
    whole, factors = pl.pallas_call(
        gather_kernel,
        out_shape=(
            pltpu.VMEM((KINDS, n * rows, columns), bf16),
            pltpu.VMEM((KINDS * n_col, LANES), f32),
        ),
        in_specs=[anywhere] * 10,
        out_specs=(local, local),
        scratch_shapes=[
            pltpu.VMEM((9, rows, columns), f32),
            pltpu.VMEM((KINDS, rows, columns), f32),
            pltpu.VMEM((2, 2, EARLY, KINDS, rows // QUARTER // EARLY, columns), f32),
            pltpu.VMEM((1, rows), f32),
            pltpu.VMEM((rows, rows), f32),
            pltpu.VMEM((KINDS * n_col, LANES), f32),
            pltpu.VMEM((KINDS * n_col, LANES), f32),
            pltpu.VMEM((3 * SIDE, KINDS * n_col, LANES), f32),
            dma((KINDS + 1,)),
            dma,
            dma,
            dma,
            dma,
            dma((4 * EARLY,)),
            dma,
            dma((N_SEM,)),
            dma,
        ],
        compiler_params=pltpu.CompilerParams(
            collective_id=0, has_side_effects=True, vmem_limit_bytes=36 * 2**20
        ),
        name="gather",
    )(*weights, gain.reshape(1, rows))
    tile = jax.ShapeDtypeStruct((n_col, LANES), f32)
    matrix = jax.ShapeDtypeStruct((n * rows, columns), bf16)
    q, k, v, tq, tk, tv = pl.pallas_call(
        store_kernel,
        out_shape=(matrix, matrix, matrix, tile, tile, tile),
        in_specs=[local, local],
        out_specs=(anywhere,) * 6,
        scratch_shapes=[dma, dma],
        compiler_params=pltpu.CompilerParams(vmem_limit_bytes=4 * 2**20),
        name="store",
    )(
        pltpu.with_memory_space_constraint(whole, pltpu.VMEM),
        pltpu.with_memory_space_constraint(factors, pltpu.VMEM),
    )
    return (q, k, v, tq.reshape(-1), tk.reshape(-1), tv.reshape(-1))


def solution(mesh):
    return jax.shard_map(
        on_device,
        mesh=mesh,
        in_specs=(P("fsdp", "model"),) * 9 + (P("fsdp"),),
        out_specs=(P(None, "model"),) * 3 + (P("model"),) * 3,
        check_vma=False,
    )
```

time: 92 us -> 87.8 us (0.954)
  Pallas kernels: 91.3 us -> 87 us
    pallas_call x1, Pallas kernels: 82.7 us -> 78.7 us  [on_device(): pl.pallas_call(gather_kernel, out_shape=(pltpu.VMEM((KINDS, n * rows, col...]
where the time goes in v3:
time: 87.8 us; the launch traced here: 87.7 us
  Pallas kernels  87 us (99%)
    pallas_call x1, Pallas kernels, on_device(): pl.pallas_call(gather_kernel, out_shape=(pltpu.VMEM((KINDS, n * rows, col...  78.7 us
    pallas_call x1, Pallas kernels, on_device(): pl.pallas_call(store_kernel, out_shape=(matrix, matrix, matrix, tile, til...  8.37 us

profile of v3, /device:TPU:1, one launch (start us, length us, event | category | flops | bytes accessed | tf_op | source)
XLA Modules:
  0.0 87.7 jit_solution(8117540494221502178)
XLA Ops:
  0.6 78.7 %gather.1 = (bf16[3,4096,1024]{2,1,0:T(8,128)(2,1)S(1)}, f32[24,128]{1,0:T(8,128)S(1)}) custom-call(f32[128,1024]{1,0:T(8,128)} %wq.1, f32[128,1024]{1,0:T(8,128)} %fq.1, f32[128,1024]{1,0:T(8,128)} %sq.1, f32[128,1024]{1,0:T(8,128)} %wk.1, f32[128,1024]{1,0:T(8,128)} %fk.1, f32[128,1024]{1,0:T(8,128)} %sk.1, f32[128,1024]{1,0:T(8,128)} %wv.1, ...), custom_call_target="tpu_custom_call" | custom-call | tf_op jit(solution)/shard_map/gather/pallas_call | solution.py:323
  79.3 8.4 %store.1 = (bf16[4096,1024]{1,0:T(8,128)(2,1)}, bf16[4096,1024]{1,0:T(8,128)(2,1)}, bf16[4096,1024]{1,0:T(8,128)(2,1)}, f32[8,128]{1,0:T(8,128)}, f32[8,128]{1,0:T(8,128)}, /*index=5*/f32[8,128]{1,0:T(8,128)}) custom-call(bf16[3,4096,1024]{2,1,0:T(8,128)(2,1)S(1)} %get-tuple-element.14.whole, f32[24,128]{1,0:T(8,128)S(1)} %get-tuple-element.15.factors), custom_call_target="tpu_custom_call" | custom-call | tf_op jit(solution)/shard_map/store/pallas_call | solution.py:357

commit v4 on v3

--- a/solution.py
+++ b/solution.py
@@ -17,13 +17,14 @@
 
 
 LAST = 2
-EARLY = 2
+EARLY = ((0, 16), (16, 8))
 
 
 def arrivals():
     names = []
-    for sign, half in ((-1, 1), (1, 0)):
-        names.append(("near", sign, half))
+    for sign in (-1, 1):
+        for half in (0, 1):
+            names.append(("near", sign, half))
     for half in (0, 1):
         names.append(("far", 0, half))
     for first in (0, -1, 1, 2):
@@ -41,7 +42,8 @@
 
 
 INDEX, N_SEM, N_LINK = arrivals()
-N_PAIR = N_LINK + 8
+EARLY_NAMES = (("near", -1, 0), ("near", 1, 1))
+N_PAIR = N_LINK + 4
 
 
 def gather_kernel(
@@ -96,15 +98,16 @@
         along_x = (color == 0) == (stage == 1)
         return device(0, sign) if along_x else device(sign, 0)
 
-    part = piece // EARLY
+    part = sum(count for _, count in EARLY)
 
     def early_copy(color, side, k):
-        low = (2 * color + side) * piece + k * part
+        start, count = EARLY[k]
+        low = (2 * color + side) * piece + start
         return pltpu.make_async_remote_copy(
-            src_ref=gained.at[:, low : low + part, :],
-            dst_ref=early.at[color, side, k],
+            src_ref=gained.at[:, low : low + count, :],
+            dst_ref=early.at[color, side, :, start : start + count, :],
             send_sem=early_send,
-            recv_sem=early_recv.at[(2 * color + side) * EARLY + k],
+            recv_sem=early_recv.at[(2 * color + side) * len(EARLY) + k],
             device_id={"fsdp": neighbour(color, 1, 1 - 2 * side)},
             device_id_type=MESH,
         )
@@ -126,10 +129,9 @@
 
     for peer in row_peers:
         sum_copy(sums, 2 * x + core, row_recv, peer).start()
-    early_copy(1, 0, 0).start()
-    early_copy(1, 1, 0).start()
-    early_copy(0, 0, 0).start()
-    early_copy(0, 1, 0).start()
+    for color in (1, 0):
+        for side in (0, 1):
+            early_copy(color, side, 0).start()
     every[2 * x + core] = sums[...]
     wait_all(every.at[0 : n_row - 1], row_recv)
     total = every[0]
@@ -138,10 +140,10 @@
     row_sums[...] = total
     for peer in column_peers:
         sum_copy(row_sums, n_row + y, column_recv, peer).start()
-    early_copy(0, 0, 1).start()
-    early_copy(0, 1, 1).start()
-    early_copy(1, 0, 1).start()
-    early_copy(1, 1, 1).start()
+    for k in range(1, len(EARLY)):
+        for color in (1, 0):
+            for side in (0, 1):
+                early_copy(color, side, k).start()
     every[n_row + y] = total
     wait_all(every.at[n_row : n_row + SIDE - 1], column_recv)
     total = every[n_row]
@@ -154,9 +156,9 @@
         dy, dx = (second, first) if color == 0 else (first, second)
         return device(dy, dx) * rows
 
-    def place(color, first, second, half):
-        at = pl.multiple_of(block_start(color, first, second) + (2 * color + half) * piece, piece)
-        return out.at[:, pl.ds(at, piece), :]
+    def place(color, first, second, half, skip=0):
+        at = block_start(color, first, second) + (2 * color + half) * piece + skip
+        return out.at[:, pl.ds(pl.multiple_of(at, 8 if skip else piece), piece - skip), :]
 
     def where(color, name):
         if name[0] == "near":
@@ -174,7 +176,8 @@
 
     def link(color, name, first, second, target, group):
         low, high = group
-        ref = place(color, first, second, name[-1]).at[low:high]
+        skip = part if name in EARLY_NAMES else 0
+        ref = place(color, first, second, name[-1], skip).at[low:high]
         return pltpu.make_async_remote_copy(
             src_ref=ref,
             dst_ref=ref,
@@ -203,6 +206,8 @@
         first, second = where(color, name)
         link(color, name, first, second, partner, group).wait_recv()
         half = name[-1]
+        if name in EARLY_NAMES:
+            send(color, ("far", 0, half), first, 0, 1, -first)
         if name[0] in ("near", "far"):
             first_axis_done(color, first, half)
         if name[0] == "near2" and (name[2], half) in ((-1, 0), (1, 1)):
@@ -215,7 +220,7 @@
 
     def scaled(color, first, half, source, low, count):
         start = block_start(color, first, 0) + (2 * color + half) * piece + low
-        at = pl.multiple_of(start, count)
+        at = pl.multiple_of(start, 8)
         for m in range(KINDS):
             for j in range(n_col):
                 cols = slice(j * LANES, (j + 1) * LANES)
@@ -226,36 +231,38 @@
 
     both = (0, 1)
     halves = (0, 1)
-    for half in halves:
-        for color in both:
-            low = (2 * color + half) * piece
-            scaled(color, 0, half, lambda m, cols: gained[m, low : low + piece, cols], 0, piece)
-    for half in halves:
-        for color in both:
-            to = 1 if half == 1 else -1
-            send(color, ("near", -to, half), 0, 0, 1, to)
-    for color in both:
-        for side in halves:
-            first = 2 * side - 1
-            for k in range(EARLY):
-                early_copy(color, side, k).wait_recv()
-                scaled(color, first, side, lambda m, cols: early[color, side, k, m, :, cols], k * part, part)
+    def own(half, color, low, count):
+        base = (2 * color + half) * piece + low
+        scaled(color, 0, half, lambda m, cols: gained[m, base : base + count, cols], low, count)
+
+    for same in (True, False):
+        for half in halves:
+            for color in both:
+                if same:
+                    own(half, color, part, piece - part)
+                else:
+                    own(half, color, 0, part)
+        for half in halves:
+            for color in both:
+                to = 1 if (half == 0) == same else -1
+                send(color, ("near", -to, half), 0, 0, 1, to)
     for half in halves:
         for color in both:
             first_axis_done(color, 0, half)
     for color in both:
         for side in halves:
-            first = 2 * side - 1
-            send(color, ("far", 0, side), first, 0, 1, -first)
-    for color in both:
-        for side in halves:
-            first_axis_done(color, 2 * side - 1, side)
+            for k, (start, count) in enumerate(EARLY):
+                early_copy(color, side, k).wait_recv()
+                rows_of = slice(start, start + count)
+                scaled(
+                    color, 2 * side - 1, side,
+                    lambda m, cols: early[color, side, m, rows_of, cols], start, count,
+                )
     for color in both:
         for half in halves:
             to_partner(color, 0, 0, half)
-            to_partner(color, 2 * half - 1, 0, half)
-
-    for name in (("near", -1, 1), ("near", 1, 0)):
+
+    for name in (*EARLY_NAMES, ("near", -1, 1), ("near", 1, 0)):
         for color in both:
             arrived(color, name)
     for name in (("near2", 0, -1, 0), ("near2", 0, 1, 1), ("near2", 0, -1, 1), ("near2", 0, 1, 0)):
@@ -281,7 +288,7 @@
                     arrived(color, (*name, half), group)
 
     wait_all(out.at[:, 0 : N_PAIR * piece, :], d2d_recv)
-    wait_all(out.at[:, 0 : (N_LINK + N_PAIR) * piece, :], all_send)
+    wait_all(out.at[:, 0 : (N_LINK + N_PAIR) * piece - 4 * part, :], all_send)
     wait_all(early, early_send)
     wait_all(every.at[0 : len(row_peers) + len(column_peers)], sum_send)
 
@@ -331,7 +338,7 @@
         scratch_shapes=[
             pltpu.VMEM((9, rows, columns), f32),
             pltpu.VMEM((KINDS, rows, columns), f32),
-            pltpu.VMEM((2, 2, EARLY, KINDS, rows // QUARTER // EARLY, columns), f32),
+            pltpu.VMEM((2, 2, KINDS, sum(count for _, count in EARLY), columns), f32),
             pltpu.VMEM((1, rows), f32),
             pltpu.VMEM((rows, rows), f32),
             pltpu.VMEM((KINDS * n_col, LANES), f32),
@@ -342,7 +349,7 @@
             dma,
             dma,
             dma,
-            dma((4 * EARLY,)),
+            dma((4 * len(EARLY),)),
             dma,
             dma((N_SEM,)),
             dma,

time: 87.8 us -> 86.8 us (0.989)
  Pallas kernels: 87 us -> 86 us
    pallas_call x1, Pallas kernels: 78.7 us -> 77.6 us  [on_device(): pl.pallas_call(gather_kernel, out_shape=(pltpu.VMEM((KINDS, n * rows, col...]
where the time goes in v4:
time: 86.8 us; the launch traced here: 86.7 us
  Pallas kernels  86 us (99%)
    pallas_call x1, Pallas kernels, on_device(): pl.pallas_call(gather_kernel, out_shape=(pltpu.VMEM((KINDS, n * rows, col...  77.6 us
    pallas_call x1, Pallas kernels, on_device(): pl.pallas_call(store_kernel, out_shape=(matrix, matrix, matrix, tile, til...  8.37 us

profile of v4, /device:TPU:1, one launch (start us, length us, event | category | flops | bytes accessed | tf_op | source)
XLA Modules:
  0.0 86.7 jit_solution(10714087200055053200)
XLA Ops:
  0.6 77.6 %gather.1 = (bf16[3,4096,1024]{2,1,0:T(8,128)(2,1)S(1)}, f32[24,128]{1,0:T(8,128)S(1)}) custom-call(f32[128,1024]{1,0:T(8,128)} %wq.1, f32[128,1024]{1,0:T(8,128)} %fq.1, f32[128,1024]{1,0:T(8,128)} %sq.1, f32[128,1024]{1,0:T(8,128)} %wk.1, f32[128,1024]{1,0:T(8,128)} %fk.1, f32[128,1024]{1,0:T(8,128)} %sk.1, f32[128,1024]{1,0:T(8,128)} %wv.1, ...), custom_call_target="tpu_custom_call" | custom-call | tf_op jit(solution)/shard_map/gather/pallas_call | solution.py:330
  78.3 8.4 %store.1 = (bf16[4096,1024]{1,0:T(8,128)(2,1)}, bf16[4096,1024]{1,0:T(8,128)(2,1)}, bf16[4096,1024]{1,0:T(8,128)(2,1)}, f32[8,128]{1,0:T(8,128)}, f32[8,128]{1,0:T(8,128)}, /*index=5*/f32[8,128]{1,0:T(8,128)}) custom-call(bf16[3,4096,1024]{2,1,0:T(8,128)(2,1)S(1)} %get-tuple-element.14.whole, f32[24,128]{1,0:T(8,128)S(1)} %get-tuple-element.15.factors), custom_call_target="tpu_custom_call" | custom-call | tf_op jit(solution)/shard_map/store/pallas_call | solution.py:364

commit v5 on v4

--- a/solution.py
+++ b/solution.py
@@ -17,32 +17,29 @@
 
 
 LAST = 2
-EARLY = ((0, 16), (16, 8))
-
-
-def arrivals():
-    names = []
-    for sign in (-1, 1):
-        for half in (0, 1):
-            names.append(("near", sign, half))
-    for half in (0, 1):
-        names.append(("far", 0, half))
+EARLY = (((0, 8), (8, 16)), ((0, 8), (8, 16)))
+EARLY_ROWS = 24
+EARLY_NAMES = (("near", -1, 0), ("near", 1, 1))
+
+
+def groups():
+    taken = [EARLY_NAMES, (("near", -1, 1), ("near", 1, 0))]
     for first in (0, -1, 1, 2):
-        for sign in (-1, 1):
-            for half in (0, 1):
-                names.append(("near2", first, sign, half))
-        for half in (0, 1):
-            names.append(("far2", first, 0, half))
-    table, at = {}, 0
-    for color in (0, 1):
-        for name in names:
-            table[(color, name)] = at
-            at += KINDS if name[:2] == ("far2", LAST) else 1
-    return table, at, 2 * len(names)
-
-
-INDEX, N_SEM, N_LINK = arrivals()
-EARLY_NAMES = (("near", -1, 0), ("near", 1, 1))
+        if first == -1:
+            taken.append((("far", 0, 0), ("far", 0, 1)))
+        taken.append((("near2", first, -1, 0), ("near2", first, 1, 1)))
+        taken.append((("near2", first, -1, 1), ("near2", first, 1, 0)))
+        if first == 1:
+            taken.append((("far2", 0, 0, 0), ("far2", 0, 0, 1)))
+    for first in (-1, 1, LAST):
+        taken.append((("far2", first, 0, 0), ("far2", first, 0, 1)))
+    return taken
+
+
+GROUPS = groups()
+GROUP_OF = {name: k for k, names in enumerate(GROUPS) for name in names}
+N_SEM = len(GROUPS) + KINDS - 1
+N_LINK = 4 * len(GROUPS)
 N_PAIR = N_LINK + 4
 
 
@@ -66,18 +63,21 @@
         return (lax.rem(y + dy + SIDE, SIDE) * SIDE + lax.rem(x + dx + SIDE, SIDE)) * 2 + on
 
     partner = device(0, 0, 1 - core)
-    row_peers = [partner] + [device(0, dx, on) for dx in (2, 1, 3) for on in (core, 1 - core)]
-    column_peers = [device(dy, 0) for dy in (2, 1, 3)]
-
-    barrier = pltpu.get_barrier_semaphore()
-    for peer in column_peers + row_peers:
-        pl.semaphore_signal(barrier, inc=1, device_id={"fsdp": peer}, device_id_type=MESH)
+    row_peers = [device(0, dx, on) for dx in (2, 1, 3) for on in (0, 1)] + [partner]
+    column_peers = [device(dy, 0, on) for dy in (2, 1, 3) for on in (0, 1)]
+
+    def wait_all(ref, sem):
+        pltpu.make_async_copy(ref, ref, sem).wait()
 
     weights = (wq, fq, sq, wk, fk, sk, wv, fv, sv)
     gain_load = pltpu.make_async_copy(gain_ref, gain_row, in_sem.at[KINDS])
     gain_load.start()
     for k, ref in enumerate(weights):
         pltpu.make_async_copy(ref, staged.at[k], in_sem.at[k // 3]).start()
+
+    barrier = pltpu.get_barrier_semaphore()
+    for peer in column_peers + row_peers:
+        pl.semaphore_signal(barrier, inc=1, device_id={"fsdp": peer}, device_id_type=MESH)
 
     gain_load.wait()
     gain_full[...] = jnp.broadcast_to(gain_row[...], (rows, rows)).T
@@ -98,21 +98,19 @@
         along_x = (color == 0) == (stage == 1)
         return device(0, sign) if along_x else device(sign, 0)
 
-    part = sum(count for _, count in EARLY)
+    part = EARLY_ROWS
 
     def early_copy(color, side, k):
-        start, count = EARLY[k]
+        start, count = EARLY[color][k]
         low = (2 * color + side) * piece + start
         return pltpu.make_async_remote_copy(
             src_ref=gained.at[:, low : low + count, :],
             dst_ref=early.at[color, side, :, start : start + count, :],
             send_sem=early_send,
-            recv_sem=early_recv.at[(2 * color + side) * len(EARLY) + k],
+            recv_sem=early_recv.at[2 * color + k],
             device_id={"fsdp": neighbour(color, 1, 1 - 2 * side)},
             device_id_type=MESH,
         )
-
-    n_row = 2 * SIDE
 
     def sum_copy(source, slot, recv_sem, target):
         return pltpu.make_async_remote_copy(
@@ -124,28 +122,43 @@
             device_id_type=MESH,
         )
 
-    def wait_all(ref, sem):
-        pltpu.make_async_copy(ref, ref, sem).wait()
-
-    for peer in row_peers:
-        sum_copy(sums, 2 * x + core, row_recv, peer).start()
+    n_row = 2 * SIDE
+    hub = 1
+    for dx in (2, 1, 3):
+        sum_copy(sums, 2 * x + core, row_recv, device(0, dx, hub)).start()
+
+    @pl.when(core != hub)
+    def _():
+        sum_copy(sums, 2 * x + core, row_recv, partner).start()
+
     for color in (1, 0):
         for side in (0, 1):
             early_copy(color, side, 0).start()
-    every[2 * x + core] = sums[...]
-    wait_all(every.at[0 : n_row - 1], row_recv)
-    total = every[0]
-    for k in range(1, n_row):
-        total = total + every[k]
-    row_sums[...] = total
-    for peer in column_peers:
-        sum_copy(row_sums, n_row + y, column_recv, peer).start()
-    for k in range(1, len(EARLY)):
-        for color in (1, 0):
-            for side in (0, 1):
-                early_copy(color, side, k).start()
-    every[n_row + y] = total
-    wait_all(every.at[n_row : n_row + SIDE - 1], column_recv)
+
+    @pl.when(core == hub)
+    def _():
+        every[2 * x + core] = sums[...]
+        wait_all(every.at[0 : n_row - 1], row_recv)
+        total = every[0]
+        for k in range(1, n_row):
+            total = total + every[k]
+        row_sums[...] = total
+        for peer in [*column_peers, partner]:
+            sum_copy(row_sums, n_row + y, column_recv, peer).start()
+        every[n_row + y] = total
+
+    for color in (0, 1):
+        for side in (0, 1):
+            early_copy(color, side, 1).start()
+
+    @pl.when(core == hub)
+    def _():
+        wait_all(every.at[n_row : n_row + SIDE - 1], column_recv)
+
+    @pl.when(core != hub)
+    def _():
+        wait_all(every.at[n_row : n_row + SIDE], column_recv)
+
     total = every[n_row]
     for k in range(1, SIDE):
         total = total + every[n_row + k]
@@ -155,6 +168,8 @@
     def block_start(color, first, second):
         dy, dx = (second, first) if color == 0 else (first, second)
         return device(dy, dx) * rows
+
+    both = (0, 1)
 
     def place(color, first, second, half, skip=0):
         at = block_start(color, first, second) + (2 * color + half) * piece + skip
@@ -169,11 +184,6 @@
             return name[1], name[2]
         return name[1], 2
 
-    def groups(name):
-        if name[:2] == ("far2", LAST):
-            return [(m, m + 1) for m in range(KINDS)]
-        return [(0, KINDS)]
-
     def link(color, name, first, second, target, group):
         low, high = group
         skip = part if name in EARLY_NAMES else 0
@@ -182,13 +192,14 @@
             src_ref=ref,
             dst_ref=ref,
             send_sem=all_send,
-            recv_sem=link_recv.at[INDEX[(color, name)] + low],
+            recv_sem=link_recv.at[GROUP_OF[name] + (low if high - low < KINDS else 0)],
             device_id={"fsdp": target},
             device_id_type=MESH,
         )
 
     def send(color, name, first, second, stage, sign):
-        for group in groups(name):
+        whole = [(m, m + 1) for m in range(KINDS)] if name[:2] == ("far2", LAST) else [(0, KINDS)]
+        for group in whole:
             link(color, name, first, second, neighbour(color, stage, sign), group).start()
 
     def to_partner(color, first, second, half, group=(0, KINDS)):
@@ -202,21 +213,36 @@
             device_id_type=MESH,
         ).start()
 
-    def arrived(color, name, group=(0, KINDS)):
+    def arrived(color, name, group):
         first, second = where(color, name)
-        link(color, name, first, second, partner, group).wait_recv()
         half = name[-1]
         if name in EARLY_NAMES:
             send(color, ("far", 0, half), first, 0, 1, -first)
-        if name[0] in ("near", "far"):
-            first_axis_done(color, first, half)
+        if name[0] == "near":
+            for to in (1, -1) if half == 0 else (-1, 1):
+                send(color, ("near2", first, -to, half), first, 0, 2, to)
         if name[0] == "near2" and (name[2], half) in ((-1, 0), (1, 1)):
             send(color, ("far2", first, 0, half), first, second, 2, -name[2])
-        to_partner(color, first, second, half, group)
-
-    def first_axis_done(color, first, half):
-        for to in (1, -1) if half == 0 else (-1, 1):
-            send(color, ("near2", first, -to, half), first, 0, 2, to)
+
+    def both_halves(first):
+        for at in (0, 1):
+            for to in (1, -1):
+                half = at if to == 1 else 1 - at
+                for color in both:
+                    send(color, ("near2", first, -to, half), first, 0, 2, to)
+
+    def take(k, group=(0, KINDS)):
+        low, high = group
+        count = 4 * (piece - part if GROUPS[k] == EARLY_NAMES else piece)
+        wait_all(out.at[low:high, 0:count, :], link_recv.at[k + (low if high - low < KINDS else 0)])
+        for name in GROUPS[k]:
+            for color in both:
+                arrived(color, name, group)
+        if GROUPS[k][0][0] == "far":
+            both_halves(2)
+        for name in GROUPS[k]:
+            for color in both:
+                to_partner(color, *where(color, name), name[-1], group)
 
     def scaled(color, first, half, source, low, count):
         start = block_start(color, first, 0) + (2 * color + half) * piece + low
@@ -229,7 +255,6 @@
                     source(m, cols) * recip[row : row + 1, :]
                 ).astype(out.dtype)
 
-    both = (0, 1)
     halves = (0, 1)
     def own(half, color, low, count):
         base = (2 * color + half) * piece + low
@@ -246,13 +271,12 @@
             for color in both:
                 to = 1 if (half == 0) == same else -1
                 send(color, ("near", -to, half), 0, 0, 1, to)
-    for half in halves:
-        for color in both:
-            first_axis_done(color, 0, half)
+    both_halves(0)
     for color in both:
-        for side in halves:
-            for k, (start, count) in enumerate(EARLY):
-                early_copy(color, side, k).wait_recv()
+        for k in range(2):
+            start, count = EARLY[color][k]
+            wait_all(early.at[color, :, :, start : start + count, :], early_recv.at[2 * color + k])
+            for side in halves:
                 rows_of = slice(start, start + count)
                 scaled(
                     color, 2 * side - 1, side,
@@ -262,35 +286,22 @@
         for half in halves:
             to_partner(color, 0, 0, half)
 
-    for name in (*EARLY_NAMES, ("near", -1, 1), ("near", 1, 0)):
-        for color in both:
-            arrived(color, name)
-    for name in (("near2", 0, -1, 0), ("near2", 0, 1, 1), ("near2", 0, -1, 1), ("near2", 0, 1, 0)):
-        for color in both:
-            arrived(color, name)
-    for name in (("far", 0, 0), ("far", 0, 1)):
-        for color in both:
-            arrived(color, name)
-    for first in (-1, 1, 2):
-        for half in ((0, 1) if first != 1 else (1, 0)):
-            for sign in (-1, 1):
-                for color in both:
-                    arrived(color, ("near2", first, sign, half))
-        if first == -1:
-            for half in halves:
-                for color in both:
-                    arrived(color, ("far2", 0, 0, half))
-    for first in (-1, 1, LAST):
-        name = ("far2", first, 0)
-        for group in groups(name):
-            for half in halves:
-                for color in both:
-                    arrived(color, (*name, half), group)
+    for k in range(len(GROUPS) - 1):
+        take(k)
+    for m in range(KINDS):
+        take(len(GROUPS) - 1, (m, m + 1))
 
     wait_all(out.at[:, 0 : N_PAIR * piece, :], d2d_recv)
     wait_all(out.at[:, 0 : (N_LINK + N_PAIR) * piece - 4 * part, :], all_send)
     wait_all(early, early_send)
-    wait_all(every.at[0 : len(row_peers) + len(column_peers)], sum_send)
+
+    @pl.when(core == hub)
+    def _():
+        wait_all(every.at[0 : SIDE - 1 + len(column_peers) + 1], sum_send)
+
+    @pl.when(core != hub)
+    def _():
+        wait_all(every.at[0:SIDE], sum_send)
 
 
 def store_kernel(whole, factors, oq, ok, ov, tq, tk, tv, sem, small):
@@ -338,7 +349,7 @@
         scratch_shapes=[
             pltpu.VMEM((9, rows, columns), f32),
             pltpu.VMEM((KINDS, rows, columns), f32),
-            pltpu.VMEM((2, 2, KINDS, sum(count for _, count in EARLY), columns), f32),
+            pltpu.VMEM((2, 2, KINDS, EARLY_ROWS, columns), f32),
             pltpu.VMEM((1, rows), f32),
             pltpu.VMEM((rows, rows), f32),
             pltpu.VMEM((KINDS * n_col, LANES), f32),
@@ -349,7 +360,7 @@
             dma,
             dma,
             dma,
-            dma((4 * len(EARLY),)),
+            dma((4,)),
             dma,
             dma((N_SEM,)),
             dma,

time: 86.8 us -> 86 us (level)
  no operation moved by 1% of the time
where the time goes in v5:
time: 86 us; the launch traced here: 85.9 us
  Pallas kernels  85.2 us (99%)
    pallas_call x1, Pallas kernels, on_device(): pl.pallas_call(gather_kernel, out_shape=(pltpu.VMEM((KINDS, n * rows, col...  76.9 us
    pallas_call x1, Pallas kernels, on_device(): pl.pallas_call(store_kernel, out_shape=(matrix, matrix, matrix, tile, til...  8.37 us

profile of v5, /device:TPU:1, one launch (start us, length us, event | category | flops | bytes accessed | tf_op | source)
XLA Modules:
  0.0 85.9 jit_solution(18062435155899210466)
XLA Ops:
  0.6 76.9 %gather.1 = (bf16[3,4096,1024]{2,1,0:T(8,128)(2,1)S(1)}, f32[24,128]{1,0:T(8,128)S(1)}) custom-call(f32[128,1024]{1,0:T(8,128)} %wq.1, f32[128,1024]{1,0:T(8,128)} %fq.1, f32[128,1024]{1,0:T(8,128)} %sq.1, f32[128,1024]{1,0:T(8,128)} %wk.1, f32[128,1024]{1,0:T(8,128)} %fk.1, f32[128,1024]{1,0:T(8,128)} %sk.1, f32[128,1024]{1,0:T(8,128)} %wv.1, ...), custom_call_target="tpu_custom_call" | custom-call | tf_op jit(solution)/shard_map/gather/pallas_call | solution.py:341
  77.5 8.4 %store.1 = (bf16[4096,1024]{1,0:T(8,128)(2,1)}, bf16[4096,1024]{1,0:T(8,128)(2,1)}, bf16[4096,1024]{1,0:T(8,128)(2,1)}, f32[8,128]{1,0:T(8,128)}, f32[8,128]{1,0:T(8,128)}, /*index=5*/f32[8,128]{1,0:T(8,128)}) custom-call(bf16[3,4096,1024]{2,1,0:T(8,128)(2,1)S(1)} %get-tuple-element.14.whole, f32[24,128]{1,0:T(8,128)S(1)} %get-tuple-element.15.factors), custom_call_target="tpu_custom_call" | custom-call | tf_op jit(solution)/shard_map/store/pallas_call | solution.py:375

commit v6 on v5

--- a/solution.py
+++ b/solution.py
@@ -17,7 +17,7 @@
 
 
 LAST = 2
-EARLY = (((0, 8), (8, 16)), ((0, 8), (8, 16)))
+EARLY = (((0, 16), (16, 8)), ((0, 8), (8, 16)))
 EARLY_ROWS = 24
 EARLY_NAMES = (("near", -1, 0), ("near", 1, 1))
 
@@ -38,7 +38,9 @@
 
 GROUPS = groups()
 GROUP_OF = {name: k for k, names in enumerate(GROUPS) for name in names}
-N_SEM = len(GROUPS) + KINDS - 1
+LAST_PARTS = ((0, 1, 0, 8), (1, 2, 0, 8), (2, 3, 0, 4), (2, 3, 4, 4))
+WHOLE = (0, KINDS, 0, 8)
+N_SEM = len(GROUPS) + len(LAST_PARTS) - 1
 N_LINK = 4 * len(GROUPS)
 N_PAIR = N_LINK + 4
 
@@ -59,10 +61,15 @@
     n_col = columns // LANES
     piece = rows // QUARTER
 
-    def device(dy, dx, on=core):
-        return (lax.rem(y + dy + SIDE, SIDE) * SIDE + lax.rem(x + dx + SIDE, SIDE)) * 2 + on
-
-    partner = device(0, 0, 1 - core)
+    ys = [lax.rem(y + d, SIDE) * (2 * SIDE) for d in range(SIDE)]
+    xs = [lax.rem(x + d, SIDE) * 2 for d in range(SIDE)]
+    table = [[ys[dy] + xs[dx] + core for dx in range(SIDE)] for dy in range(SIDE)]
+
+    def device(dy, dx, on=None):
+        here = table[dy % SIDE][dx % SIDE]
+        return here if on is None else here - core + on
+
+    partner = me + 1 - 2 * core
     row_peers = [device(0, dx, on) for dx in (2, 1, 3) for on in (0, 1)] + [partner]
     column_peers = [device(dy, 0, on) for dy in (2, 1, 3) for on in (0, 1)]
 
@@ -184,26 +191,36 @@
             return name[1], name[2]
         return name[1], 2
 
+    def cut(color, first, second, half, group):
+        low, high, start, count = group
+        at = block_start(color, first, second) + (2 * color + half) * piece + start * (piece // 8)
+        rows_of = pl.ds(pl.multiple_of(at, 16), count * (piece // 8))
+        return out.at[low:high, rows_of, :]
+
     def link(color, name, first, second, target, group):
-        low, high = group
-        skip = part if name in EARLY_NAMES else 0
-        ref = place(color, first, second, name[-1], skip).at[low:high]
+        k = GROUP_OF[name]
+        if name in EARLY_NAMES:
+            ref = place(color, first, second, name[-1], part)
+        elif group == WHOLE:
+            ref = place(color, first, second, name[-1])
+        else:
+            ref = cut(color, first, second, name[-1], group)
+            k += LAST_PARTS.index(group)
         return pltpu.make_async_remote_copy(
             src_ref=ref,
             dst_ref=ref,
             send_sem=all_send,
-            recv_sem=link_recv.at[GROUP_OF[name] + (low if high - low < KINDS else 0)],
+            recv_sem=link_recv.at[k],
             device_id={"fsdp": target},
             device_id_type=MESH,
         )
 
     def send(color, name, first, second, stage, sign):
-        whole = [(m, m + 1) for m in range(KINDS)] if name[:2] == ("far2", LAST) else [(0, KINDS)]
-        for group in whole:
+        for group in LAST_PARTS if name[:2] == ("far2", LAST) else (WHOLE,):
             link(color, name, first, second, neighbour(color, stage, sign), group).start()
 
-    def to_partner(color, first, second, half, group=(0, KINDS)):
-        ref = place(color, first, second, half).at[group[0] : group[1]]
+    def to_partner(color, first, second, half, group=WHOLE):
+        ref = cut(color, first, second, half, group)
         pltpu.make_async_remote_copy(
             src_ref=ref,
             dst_ref=ref,
@@ -231,10 +248,11 @@
                 for color in both:
                     send(color, ("near2", first, -to, half), first, 0, 2, to)
 
-    def take(k, group=(0, KINDS)):
-        low, high = group
-        count = 4 * (piece - part if GROUPS[k] == EARLY_NAMES else piece)
-        wait_all(out.at[low:high, 0:count, :], link_recv.at[k + (low if high - low < KINDS else 0)])
+    def take(k, group=WHOLE):
+        low, high, _, count = group
+        count = 4 * (piece - part if GROUPS[k] == EARLY_NAMES else count * (piece // 8))
+        sem = link_recv.at[k if group == WHOLE else k + LAST_PARTS.index(group)]
+        wait_all(out.at[low:high, 0:count, :], sem)
         for name in GROUPS[k]:
             for color in both:
                 arrived(color, name, group)
@@ -288,8 +306,8 @@
 
     for k in range(len(GROUPS) - 1):
         take(k)
-    for m in range(KINDS):
-        take(len(GROUPS) - 1, (m, m + 1))
+    for group in LAST_PARTS:
+        take(len(GROUPS) - 1, group)
 
     wait_all(out.at[:, 0 : N_PAIR * piece, :], d2d_recv)
     wait_all(out.at[:, 0 : (N_LINK + N_PAIR) * piece - 4 * part, :], all_send)

time: 86 us -> 85.8 us (level)
  no operation moved by 1% of the time
where the time goes in v6:
time: 85.8 us; the launch traced here: 85.7 us
  Pallas kernels  85.1 us (99%)
    pallas_call x1, Pallas kernels, on_device(): pl.pallas_call(gather_kernel, out_shape=(pltpu.VMEM((KINDS, n * rows, col...  76.7 us
    pallas_call x1, Pallas kernels, on_device(): pl.pallas_call(store_kernel, out_shape=(matrix, matrix, matrix, tile, til...  8.37 us

profile of v6, /device:TPU:1, one launch (start us, length us, event | category | flops | bytes accessed | tf_op | source)
XLA Modules:
  0.0 85.7 jit_solution(6149508644481022431)
XLA Ops:
  0.6 76.7 %gather.1 = (bf16[3,4096,1024]{2,1,0:T(8,128)(2,1)S(1)}, f32[24,128]{1,0:T(8,128)S(1)}) custom-call(f32[128,1024]{1,0:T(8,128)} %wq.1, f32[128,1024]{1,0:T(8,128)} %fq.1, f32[128,1024]{1,0:T(8,128)} %sq.1, f32[128,1024]{1,0:T(8,128)} %wk.1, f32[128,1024]{1,0:T(8,128)} %fk.1, f32[128,1024]{1,0:T(8,128)} %sk.1, f32[128,1024]{1,0:T(8,128)} %wv.1, ...), custom_call_target="tpu_custom_call" | custom-call | tf_op jit(solution)/shard_map/gather/pallas_call | solution.py:359
  77.3 8.4 %store.1 = (bf16[4096,1024]{1,0:T(8,128)(2,1)}, bf16[4096,1024]{1,0:T(8,128)(2,1)}, bf16[4096,1024]{1,0:T(8,128)(2,1)}, f32[8,128]{1,0:T(8,128)}, f32[8,128]{1,0:T(8,128)}, /*index=5*/f32[8,128]{1,0:T(8,128)}) custom-call(bf16[3,4096,1024]{2,1,0:T(8,128)(2,1)S(1)} %get-tuple-element.14.whole, f32[24,128]{1,0:T(8,128)S(1)} %get-tuple-element.15.factors), custom_call_target="tpu_custom_call" | custom-call | tf_op jit(solution)/shard_map/store/pallas_call | solution.py:393

commit v7 on v6

--- a/solution.py
+++ b/solution.py
@@ -83,8 +83,22 @@
         pltpu.make_async_copy(ref, staged.at[k], in_sem.at[k // 3]).start()
 
     barrier = pltpu.get_barrier_semaphore()
-    for peer in column_peers + row_peers:
+    hub = 1
+
+    def greet(peer):
         pl.semaphore_signal(barrier, inc=1, device_id={"fsdp": peer}, device_id_type=MESH)
+
+    for dy, dx in ((2, 0), (0, 2)):
+        greet(device(dy, dx, 1 - core))
+
+        @pl.when(core == hub)
+        def _():
+            greet(device(dy, dx))
+
+    for dy, dx in ((1, 0), (3, 0), (0, 1), (0, 3)):
+        greet(device(dy, dx, 1 - core))
+        greet(device(dy, dx))
+    greet(partner)
 
     gain_load.wait()
     gain_full[...] = jnp.broadcast_to(gain_row[...], (rows, rows)).T
@@ -99,7 +113,16 @@
             gained[m, :, at] = value
             sums[m * n_col + j : m * n_col + j + 1, :] = jnp.sum(jnp.abs(value), axis=0, keepdims=True)
 
-    pl.semaphore_wait(barrier, len(row_peers) + len(column_peers))
+    near_peers = len(row_peers) + len(column_peers) - 2
+
+    @pl.when(core == hub)
+    def _():
+        pl.semaphore_wait(barrier, near_peers + 2)
+
+    @pl.when(core != hub)
+    def _():
+        pl.semaphore_wait(barrier, near_peers)
+
 
     def neighbour(color, stage, sign):
         along_x = (color == 0) == (stage == 1)
@@ -130,7 +153,6 @@
         )
 
     n_row = 2 * SIDE
-    hub = 1
     for dx in (2, 1, 3):
         sum_copy(sums, 2 * x + core, row_recv, device(0, dx, hub)).start()
 

time: 85.8 us -> 85.8 us (level)
  no operation moved by 1% of the time
where the time goes in v7:
time: 85.8 us; the launch traced here: 85.7 us
  Pallas kernels  85.1 us (99%)
    pallas_call x1, Pallas kernels, on_device(): pl.pallas_call(gather_kernel, out_shape=(pltpu.VMEM((KINDS, n * rows, col...  76.7 us
    pallas_call x1, Pallas kernels, on_device(): pl.pallas_call(store_kernel, out_shape=(matrix, matrix, matrix, tile, til...  8.37 us

profile of v7, /device:TPU:1, one launch (start us, length us, event | category | flops | bytes accessed | tf_op | source)
XLA Modules:
  0.0 85.7 jit_solution(10715802904249746743)
XLA Ops:
  0.6 76.7 %gather.1 = (bf16[3,4096,1024]{2,1,0:T(8,128)(2,1)S(1)}, f32[24,128]{1,0:T(8,128)S(1)}) custom-call(f32[128,1024]{1,0:T(8,128)} %wq.1, f32[128,1024]{1,0:T(8,128)} %fq.1, f32[128,1024]{1,0:T(8,128)} %sq.1, f32[128,1024]{1,0:T(8,128)} %wk.1, f32[128,1024]{1,0:T(8,128)} %fk.1, f32[128,1024]{1,0:T(8,128)} %sk.1, f32[128,1024]{1,0:T(8,128)} %wv.1, ...), custom_call_target="tpu_custom_call" | custom-call | tf_op jit(solution)/shard_map/gather/pallas_call | solution.py:381
  77.3 8.4 %store.1 = (bf16[4096,1024]{1,0:T(8,128)(2,1)}, bf16[4096,1024]{1,0:T(8,128)(2,1)}, bf16[4096,1024]{1,0:T(8,128)(2,1)}, f32[8,128]{1,0:T(8,128)}, f32[8,128]{1,0:T(8,128)}, /*index=5*/f32[8,128]{1,0:T(8,128)}) custom-call(bf16[3,4096,1024]{2,1,0:T(8,128)(2,1)S(1)} %get-tuple-element.14.whole, f32[24,128]{1,0:T(8,128)S(1)} %get-tuple-element.15.factors), custom_call_target="tpu_custom_call" | custom-call | tf_op jit(solution)/shard_map/store/pallas_call | solution.py:415

commit v8 on v6

--- a/solution.py
+++ b/solution.py
@@ -38,7 +38,7 @@
 
 GROUPS = groups()
 GROUP_OF = {name: k for k, names in enumerate(GROUPS) for name in names}
-LAST_PARTS = ((0, 1, 0, 8), (1, 2, 0, 8), (2, 3, 0, 4), (2, 3, 4, 4))
+LAST_PARTS = ((0, 2, 0, 8), (2, 3, 0, 4), (2, 3, 4, 2), (2, 3, 6, 2))
 WHOLE = (0, KINDS, 0, 8)
 N_SEM = len(GROUPS) + len(LAST_PARTS) - 1
 N_LINK = 4 * len(GROUPS)
@@ -194,7 +194,7 @@
     def cut(color, first, second, half, group):
         low, high, start, count = group
         at = block_start(color, first, second) + (2 * color + half) * piece + start * (piece // 8)
-        rows_of = pl.ds(pl.multiple_of(at, 16), count * (piece // 8))
+        rows_of = pl.ds(pl.multiple_of(at, 8), count * (piece // 8))
         return out.at[low:high, rows_of, :]
 
     def link(color, name, first, second, target, group):
@@ -278,6 +278,13 @@
         base = (2 * color + half) * piece + low
         scaled(color, 0, half, lambda m, cols: gained[m, base : base + count, cols], low, count)
 
+    waiting = []
+
+    def flush(keep):
+        while len(waiting) > keep:
+            color, half, to = waiting.pop(0)
+            send(color, ("near", -to, half), 0, 0, 1, to)
+
     for same in (True, False):
         for half in halves:
             for color in both:
@@ -285,10 +292,9 @@
                     own(half, color, part, piece - part)
                 else:
                     own(half, color, 0, part)
-        for half in halves:
-            for color in both:
-                to = 1 if (half == 0) == same else -1
-                send(color, ("near", -to, half), 0, 0, 1, to)
+                waiting.append((color, half, 1 if (half == 0) == same else -1))
+                flush(1)
+    flush(0)
     both_halves(0)
     for color in both:
         for k in range(2):

time: 85.8 us -> 85.7 us (level)
  no operation moved by 1% of the time
where the time goes in v8:
time: 85.7 us; the launch traced here: 85.6 us
  Pallas kernels  85 us (99%)
    pallas_call x1, Pallas kernels, on_device(): pl.pallas_call(gather_kernel, out_shape=(pltpu.VMEM((KINDS, n * rows, col...  76.6 us
    pallas_call x1, Pallas kernels, on_device(): pl.pallas_call(store_kernel, out_shape=(matrix, matrix, matrix, tile, til...  8.37 us

profile of v8, /device:TPU:1, one launch (start us, length us, event | category | flops | bytes accessed | tf_op | source)
XLA Modules:
  0.0 85.6 jit_solution(15710769115935119693)
XLA Ops:
  0.6 76.6 %gather.1 = (bf16[3,4096,1024]{2,1,0:T(8,128)(2,1)S(1)}, f32[24,128]{1,0:T(8,128)S(1)}) custom-call(f32[128,1024]{1,0:T(8,128)} %wq.1, f32[128,1024]{1,0:T(8,128)} %fq.1, f32[128,1024]{1,0:T(8,128)} %sq.1, f32[128,1024]{1,0:T(8,128)} %wk.1, f32[128,1024]{1,0:T(8,128)} %fk.1, f32[128,1024]{1,0:T(8,128)} %sk.1, f32[128,1024]{1,0:T(8,128)} %wv.1, ...), custom_call_target="tpu_custom_call" | custom-call | tf_op jit(solution)/shard_map/gather/pallas_call | solution.py:365
  77.2 8.4 %store.1 = (bf16[4096,1024]{1,0:T(8,128)(2,1)}, bf16[4096,1024]{1,0:T(8,128)(2,1)}, bf16[4096,1024]{1,0:T(8,128)(2,1)}, f32[8,128]{1,0:T(8,128)}, f32[8,128]{1,0:T(8,128)}, /*index=5*/f32[8,128]{1,0:T(8,128)}) custom-call(bf16[3,4096,1024]{2,1,0:T(8,128)(2,1)S(1)} %get-tuple-element.14.whole, f32[24,128]{1,0:T(8,128)S(1)} %get-tuple-element.15.factors), custom_call_target="tpu_custom_call" | custom-call | tf_op jit(solution)/shard_map/store/pallas_call | solution.py:399
